TPU v7x, 16 devices: a whole 2x2x2 slice. The times are simulated.
16 devices in a mesh: dp: 2 (over z), wg: 8 (over y, x, core).
Axes of the slice: x: 2, y: 2, z: 2, core: 2. Of those that a mesh axis runs over, the one named last changes fastest.
Arguments:
- hidden: bfloat16 [256, 32, 4096], P(('dp', 'wg')), parts along dimension 0
- seq_lens: int32 [256], P(('dp', 'wg')), parts along dimension 0
- route_idx: int32 [8192, 2], P(('dp', 'wg')), parts along dimension 0
- g_attn_in: bfloat16 [4096], P('wg')
- w_query: bfloat16 [4096, 4096], P('wg')
- w_key: bfloat16 [4096, 1024], P('wg')
- w_value: bfloat16 [4096, 1024], P('wg')
- w_attn_out: bfloat16 [4096, 4096], P('wg')
- g_attn_out: bfloat16 [4096], P('wg')
- g_moe_in: bfloat16 [4096], P('wg')
- w_router: bfloat16 [4096, 8], P('wg')
- w_gate: bfloat16 [8, 4096, 1024], P(None, 'wg')
- w_up: bfloat16 [8, 4096, 1024], P(None, 'wg')
- w_down: bfloat16 [8, 1024, 4096], P(None, 'wg')
- g_moe_out: bfloat16 [4096], P('wg')
Outputs:
- output 1: bfloat16 [256, 32, 4096], P(('dp', 'wg')), parts along dimension 0
- output 2: bfloat16 [256, 32, 8, 128], P(('dp', 'wg')), parts along dimension 0
- output 3: bfloat16 [256, 32, 8, 128], P(('dp', 'wg')), parts along dimension 0
There are 2 independent parts. A program takes and returns all parts, laid end to end along the dimension named above; an argument that names none is the same for every part.
All inputs are finite; a program needn't handle non-finite values.
Results may differ from a plain program's by a relative error of at most 0.02.
Values are sent between devices in bfloat16 or wider.
A program may use at most 1 GiB of HBM per device.

v0:
```python
import functools
import jax
import jax.numpy as jnp
from jax import lax
from jax.sharding import PartitionSpec as P

HEAD_DIM = 128
SOFT_CAP = 30.0
NORM_EPS = 1e-5
ROPE_BASE = 10000.0
ATTN_SCALE = HEAD_DIM ** -0.5


def dot_f32(left_op, right_op):
    return jnp.dot(left_op, right_op, preferred_element_type=jnp.float32)


def rms_norm(values, gain_vec):
    values_f32 = values.astype(jnp.float32)
    inv_rms = lax.rsqrt(jnp.mean(values_f32 * values_f32, axis=-1, keepdims=True) + NORM_EPS)
    return values_f32 * inv_rms * gain_vec.astype(jnp.float32)


def rope_tables(seq_len):
    half_dim = HEAD_DIM // 2
    inv_freq = ROPE_BASE ** (-jnp.arange(half_dim, dtype=jnp.float32) * (2.0 / HEAD_DIM))
    angles = jnp.arange(seq_len, dtype=jnp.float32)[:, None] * inv_freq[None, :]
    return jnp.cos(angles)[:, None, :], jnp.sin(angles)[:, None, :]


def apply_rope(values, cos_t, sin_t):
    half_dim = HEAD_DIM // 2
    values_f32 = values.astype(jnp.float32)
    first_half = values_f32[..., :half_dim]
    second_half = values_f32[..., half_dim:]
    return jnp.concatenate([first_half * cos_t - second_half * sin_t, second_half * cos_t + first_half * sin_t], axis=-1).astype(jnp.bfloat16)


def attend_prompt(operands):
    q_rows, k_rows, v_rows, length = operands
    positions = jnp.arange(q_rows.shape[0])
    scores = jnp.einsum('qkgd,skd->kgqs', q_rows, k_rows, preferred_element_type=jnp.float32) * ATTN_SCALE
    scores = SOFT_CAP * jnp.tanh(scores / SOFT_CAP)
    allowed = (positions[None, :] <= positions[:, None]) & (positions[None, :] < length)
    scores = jnp.where(allowed, scores, -1e30)
    attn_probs = jax.nn.softmax(scores, axis=-1).astype(jnp.bfloat16)
    return jnp.einsum('kgqs,skd->qkgd', attn_probs, v_rows, preferred_element_type=jnp.float32).astype(jnp.bfloat16)


def attend_rows(q_proj, k_proj, v_proj, seq_lens):
    n_prompts = seq_lens.shape[0]
    seq_len = q_proj.shape[0] // n_prompts
    n_heads = q_proj.shape[1] // HEAD_DIM
    n_kv = k_proj.shape[1] // HEAD_DIM
    cos_t, sin_t = rope_tables(seq_len)
    q_rope = apply_rope(q_proj.reshape(n_prompts, seq_len, n_heads, HEAD_DIM), cos_t, sin_t)
    k_rope = apply_rope(k_proj.reshape(n_prompts, seq_len, n_kv, HEAD_DIM), cos_t, sin_t)
    v_heads = v_proj.reshape(n_prompts, seq_len, n_kv, HEAD_DIM)
    q_groups = q_rope.reshape(n_prompts, seq_len, n_kv, n_heads // n_kv, HEAD_DIM)
    context = lax.map(attend_prompt, (q_groups, k_rope, v_heads, seq_lens))
    return context.reshape(n_prompts * seq_len, n_heads * HEAD_DIM), k_rope, v_heads


def moe_rows(h_moe, gate_probs, route_idx, w_gate, w_up, w_down):
    top_k = route_idx.shape[1]
    flat_ids = route_idx.reshape(-1)
    pair_order = jnp.argsort(flat_ids, stable=True)
    counts = jnp.bincount(flat_ids, length=w_gate.shape[0]).astype(jnp.int32)
    sorted_rows = jnp.take(h_moe, pair_order // top_k, axis=0)
    gate_act = lax.ragged_dot(sorted_rows, w_gate, counts, preferred_element_type=jnp.float32)
    up_act = lax.ragged_dot(sorted_rows, w_up, counts, preferred_element_type=jnp.float32)
    inner_act = (jax.nn.gelu(gate_act) * up_act).astype(jnp.bfloat16)
    expert_out = lax.ragged_dot(inner_act, w_down, counts, preferred_element_type=jnp.float32)
    pair_out = jnp.take(expert_out, jnp.argsort(pair_order), axis=0).reshape(h_moe.shape[0], top_k, -1)
    return jnp.sum(gate_probs[:, :, None] * pair_out, axis=1)


def solution(mesh):
    row_spec = P(('dp', 'wg'))
    dim0_spec = P('wg', None)
    dim1_spec = P(None, 'wg', None)
    gather_dim0 = functools.partial(lax.all_gather, axis_name='wg', axis=0, tiled=True)
    gather_dim1 = functools.partial(lax.all_gather, axis_name='wg', axis=1, tiled=True)

    def device_fn(hidden, seq_lens, route_idx, g_attn_in, w_query, w_key, w_value, w_attn_out, g_attn_out, g_moe_in, w_router, w_gate, w_up, w_down, g_moe_out):
        n_prompts, seq_len, d_model = hidden.shape
        tok_rows = hidden.reshape(n_prompts * seq_len, d_model)
        h_attn = rms_norm(tok_rows, gather_dim0(g_attn_in)).astype(jnp.bfloat16)
        q_proj = dot_f32(h_attn, gather_dim0(w_query)).astype(jnp.bfloat16)
        k_proj = dot_f32(h_attn, gather_dim0(w_key)).astype(jnp.bfloat16)
        v_proj = dot_f32(h_attn, gather_dim0(w_value)).astype(jnp.bfloat16)
        context_rows, k_rope, v_heads = attend_rows(q_proj, k_proj, v_proj, seq_lens)
        attn_out = dot_f32(context_rows, gather_dim0(w_attn_out))
        mid_rows = (tok_rows.astype(jnp.float32) + rms_norm(attn_out, gather_dim0(g_attn_out))).astype(jnp.bfloat16)
        h_moe = rms_norm(mid_rows, gather_dim0(g_moe_in)).astype(jnp.bfloat16)
        router_probs = jax.nn.softmax(dot_f32(h_moe, gather_dim0(w_router)), axis=-1)
        gate_probs = jnp.take_along_axis(router_probs, route_idx, axis=1)
        moe_out = moe_rows(h_moe, gate_probs, route_idx, gather_dim1(w_gate), gather_dim1(w_up), gather_dim1(w_down))
        y_rows = (mid_rows.astype(jnp.float32) + rms_norm(moe_out, gather_dim0(g_moe_out))).astype(jnp.bfloat16)
        return y_rows.reshape(hidden.shape), k_rope, v_heads

    return jax.shard_map(
        device_fn,
        mesh=mesh,
        in_specs=(row_spec, row_spec, row_spec, P('wg'), dim0_spec, dim0_spec, dim0_spec, dim0_spec, P('wg'), P('wg'), dim0_spec, dim1_spec, dim1_spec, dim1_spec, P('wg')),
        out_specs=(row_spec, row_spec, row_spec),
        check_vma=False,
    )
```

profile of v0, /device:TPU:0, one launch (start us, length us, event | category | flops | bytes accessed | tf_op | source)
XLA Modules:
  0.0 1474.7 jit_solution(15308421902481415260)
XLA Ops:
  12.0 10.6 all-gather
  22.6 3.1 fusion.26
  25.8 8.9 all-gather.1
  34.7 8.0 all-gather.2
  43.7 8.1 scatter_custom_fusion
  53.4 4.4 sort.34
  57.7 4.4 sort.35
  63.0 8.8 all-gather.3
  72.4 8.5 all_gather.43
  82.7 5.8 fusion.28
  88.4 8.6 convert_bitcast_fusion.1
  97.5 18.4 %all-gather.12.cloned.1.call-done = bf16[4096,1024]{1,0:T(8,128)(2,1)} async-done(((bf16[512,1024]{1,0:T(8,128)(2,1)}), bf16[4096,1024]{1,0:T(8,128)(2,1)}) %all-gather.12.cloned.1.call-update) | async-done | bytes 8388624 | tf_op jit(solution)/shard_map/all_gather | solution.py:91
  116.0 9.1 fusion.39
  126.8 148.1 %all-gather.16.cloned.1.call-done = bf16[4096,4096]{1,0:T(8,128)(2,1)} async-done(((bf16[512,4096]{1,0:T(8,128)(2,1)}), bf16[4096,4096]{1,0:T(8,128)(2,1)}) %all-gather.16.cloned.1.call-update) | async-done | bytes 33554448 | tf_op jit(solution)/shard_map/all_gather | solution.py:89
  274.9 22.6 %convert_bitcast_fusion = f32[64,8,32,128]{3,1,2,0:T(8,128)S(1)} fusion(bf16[512,4096]{1,0:T(8,128)(2,1)} %fusion.28, bf16[4096,4096]{1,0:T(8,128)(2,1)} %all-gather.16.cloned.1.call-done), kind=kOutput, calls=%fused_computation.46 | convolution fusion | flops 17184063488 | bytes 46137344 | tf_op jit(solution)/shard_map/dot_general | solution.py:15
  297.5 1.8 copy.70
  299.3 3.0 subtract_convert_fusion
  302.3 1.8 copy.51
  304.1 1.8 copy.52
  305.9 3.7 pad_maximum_fusion
  309.6 64.0 %while.12 = (s32[]{:T(128)}, bf16[16,32,8,4,128]{4,3,2,1,0:T(4,128)(2,1)}, bf16[16,32,8,128]{3,2,1,0:T(8,128)(2,1)S(1)}, s32[16]{0:T(128)S(1)}, bf16[16,32,8,128...) while((s32[]{:T(128)}, bf16[16,32,8,4,128]{4,3,2,1,0:T(4,128)(2,1)}, ...), condition=%wide.region_4.5_spmd, body=%wide.region_1.4_spmd.sunk | while | flops 17139776 | bytes 1715361 | solution.py:60
  310.9 1.5 fusion.70
  314.9 1.5 fusion.70
  326.9 1.5 fusion.70
  338.9 1.5 fusion.70
  350.9 1.5 fusion.70
  363.0 1.5 fusion.70
  373.6 8.2 reshape.173
  381.8 51.8 %all-gather.18.cloned.1.call-done = bf16[4096,4096]{1,0:T(8,128)(2,1)} async-done(((bf16[512,4096]{1,0:T(8,128)(2,1)}), bf16[4096,4096]{1,0:T(8,128)(2,1)}) %all-gather.18.cloned.1.call-update) | async-done | bytes 33554448 | tf_op jit(solution)/shard_map/all_gather | solution.py:93
  433.6 23.0 %multiply_reduce_fusion.2 = (f32[512]{0:T(512)S(1)}, f32[512,4096]{1,0:T(8,128)S(1)}) fusion(bf16[512,4096]{1,0:T(8,128)(2,1)} %reshape.173, bf16[4096,4096]{1,0:T(8,128)(2,1)} %all-gather.18.cloned.1.call-done), kind=kOutput, calls=%fused_computation.48 | convolution fusion | flops 17184063488 | bytes 46139392 | tf_op jit(solution)/shard_map/dot_general | solution.py:15
  456.7 2.7 fusion.22
  459.5 1.7 fusion.24
  463.2 6.5 gather_fusion.2
  470.2 17.8 %gather_fusion = bf16[1024,4096]{1,0:T(8,128)(2,1)} fusion(bf16[512,4096]{1,0:T(8,128)(2,1)} %copy-done, s32[1024]{0:T(1024)S(1)} %copy-done.11), kind=kCustom, calls=%fused_computation | custom fusion | bytes 16781312 | tf_op jit(solution)/shard_map/jit(_take)/gather | solution.py:69
  488.1 7.4 broadcast_select_fusion
  495.5 238.9 %all-gather.20.cloned.1.call-done = bf16[8,4096,1024]{2,1,0:T(8,128)(2,1)} async-done(((bf16[8,512,1024]{2,1,0:T(8,128)(2,1)}), bf16[8,4096,1024]{2,1,0:T(8,128)(2,1)}) %all-gather.20.cloned.1.call-update) | async-done | bytes 67108880 | tf_op jit(solution)/shard_map/all_gather | solution.py:98
  734.4 37.8 %ragged-dot-none.2 = f32[1024,1024]{1,0:T(8,128)} custom-call(s32[1]{0:T(128)} %get-tuple-element.85, s32[9]{0:T(128)} %get-tuple-element.86, s32[11]{0:T(128)} %get-tuple-element.87, s32[11]{0:T(128)} %get-tuple-element.88, s32[1]{0:T(128)} %get-tuple-element.85, bf16[1024,4096]{1,0:T(8,128)(2,1)} %broadcast_select_fusion, ...), custom_call_target="tpu_custom_call" | custom-call | flops 8589934592 | bytes 79691808 | tf_op jit(solution)/shard_map/ragged_dot_general/ragged-dot-none
  772.2 263.0 %all-gather.22.cloned.1.call-done = bf16[8,4096,1024]{2,1,0:T(8,128)(2,1)} async-done(((bf16[8,512,1024]{2,1,0:T(8,128)(2,1)}), bf16[8,4096,1024]{2,1,0:T(8,128)(2,1)}) %all-gather.22.cloned.1.call-update) | async-done | bytes 67108880 | tf_op jit(solution)/shard_map/all_gather | solution.py:98
  1035.2 37.8 %ragged-dot-none.1 = f32[1024,1024]{1,0:T(8,128)} custom-call(s32[1]{0:T(128)} %get-tuple-element.85, s32[9]{0:T(128)} %get-tuple-element.86, s32[11]{0:T(128)} %get-tuple-element.87, s32[11]{0:T(128)} %get-tuple-element.88, s32[1]{0:T(128)} %get-tuple-element.85, bf16[1024,4096]{1,0:T(8,128)(2,1)} %broadcast_select_fusion, ...), custom_call_target="tpu_custom_call" | custom-call | flops 8589934592 | bytes 79691808 | tf_op jit(solution)/shard_map/ragged_dot_general/ragged-dot-none
  1073.0 5.2 fusion.38
  1078.2 257.9 %all-gather.24.cloned.1.call-done = bf16[8,1024,4096]{2,1,0:T(8,128)(2,1)} async-done(((bf16[8,128,4096]{2,1,0:T(8,128)(2,1)}), bf16[8,1024,4096]{2,1,0:T(8,128)(2,1)}) %all-gather.24.cloned.1.call-update) | async-done | bytes 67108880 | tf_op jit(solution)/shard_map/all_gather | solution.py:98
  1336.1 42.0 %ragged-dot-none = f32[1024,4096]{1,0:T(8,128)} custom-call(s32[1]{0:T(128)} %get-tuple-element.85, s32[9]{0:T(128)} %get-tuple-element.86, s32[11]{0:T(128)} %get-tuple-element.87, s32[11]{0:T(128)} %get-tuple-element.88, s32[1]{0:T(128)} %get-tuple-element.85, bf16[1024,1024]{1,0:T(8,128)(2,1)} %fusion.38, bf16[8,1024,4096]{2,1,0:T(8,128)(2,1)} %all-gather.24.cloned.1.call-done), custom_call_target="tpu_custom_call" | custom-call | flops 8589934592 | bytes 85983264 | tf_op jit(solution)/shard_map/ragged_dot_general/ragged-dot-none
  1378.1 20.4 %gather_fusion.1 = f32[1024,4096]{1,0:T(8,128)} fusion(f32[1024,4096]{1,0:T(8,128)} %ragged-dot-none, s32[1024]{0:T(1024)S(1)} %copy-done.10), kind=kCustom, calls=%fused_computation.1 | custom fusion | bytes 33558528 | tf_op jit(solution)/shard_map/jit(_take)/gather | solution.py:74
  1398.5 20.1 %gather.17 = f32[512,2,4096]{2,1,0:T(2,128)} reshape(f32[1024,4096]{1,0:T(8,128)} %gather_fusion.1) | data formatting | bytes 33554432 | tf_op jit(solution)/shard_map/jit(_take)/gather | solution.py:74
  1418.5 37.0 %multiply_reduce_fusion = f32[512,4096]{1,0:T(8,128)} fusion(f32[512,2,4096]{2,1,0:T(2,128)} %gather.17, pred[512,2]{1,0:T(8,128)(4,1)S(1)} %copy-done.6, f32[512,2]{1,0:T(8,128)S(1)} %copy.58), kind=kLoop, calls=%fused_computation.31 | loop fusion | flops 10485760 | bytes 25170944 | tf_op jit(solution)/shard_map/reduce_sum | solution.py:75
  1455.5 4.2 multiply_reduce_fusion.1
  1459.7 1.6 copy-done.1
  1461.3 6.1 fusion.25
  (202 shorter events, 69.9 us)
Async XLA Ops:
  7.2 81.3 %all-gather.14.cloned.1.call-start = ((), (), s32[]{:S(2)}) async-start(), calls=%async_computation.1 | async-start | bytes 9437184 | tf_op jit(solution)/shard_map/all_gather | solution.py:90
  7.9 108.0 %all-gather.12.cloned.1.call-start = ((), (), s32[]{:S(2)}) async-start(), calls=%async_computation | async-start | bytes 9437184 | tf_op jit(solution)/shard_map/all_gather | solution.py:91
  8.6 266.2 %all-gather.16.cloned.1.call-start = ((), (), s32[]{:S(2)}) async-start(), calls=%async_computation.2 | async-start | bytes 37748736 | tf_op jit(solution)/shard_map/all_gather | solution.py:89
  9.4 424.2 %all-gather.18.cloned.1.call-start = ((), (), s32[]{:S(2)}) async-start(), calls=%async_computation.3 | async-start | bytes 37748736 | tf_op jit(solution)/shard_map/all_gather | solution.py:93
  10.0 724.4 %all-gather.20.cloned.1.call-start = ((), (), s32[]{:S(2)}) async-start(), calls=%async_computation.4 | async-start | bytes 75497472 | tf_op jit(solution)/shard_map/all_gather | solution.py:98
  10.5 1.4 copy-start.14
  10.6 1024.6 %all-gather.22.cloned.1.call-start = ((), (), s32[]{:S(2)}) async-start(), calls=%async_computation.5 | async-start | bytes 75497472 | tf_op jit(solution)/shard_map/all_gather | solution.py:98
  11.1 14.6 copy-start.15
  11.1 23.5 %copy-start.16 = (bf16[512]{0:T(512)(128)(2,1)S(1)}, bf16[512]{0:T(512)(128)(2,1)}, u32[]{:S(2)}) copy-start(bf16[512]{0:T(512)(128)(2,1)} %param.26) | copy-start | bytes 3076
  11.2 31.5 %copy-start.8 = (s32[512,2]{0,1:T(2,128)S(1)}, s32[512,2]{0,1:T(2,128)}, u32[]{:S(2)}) copy-start(s32[512,2]{0,1:T(2,128)} %param.19) | copy-start | bytes 12292
  11.2 51.8 %copy-start.17 = (bf16[512]{0:T(512)(128)(2,1)S(1)}, bf16[512]{0:T(512)(128)(2,1)}, u32[]{:S(2)}) copy-start(bf16[512]{0:T(512)(128)(2,1)} %param.31) | copy-start | bytes 3076
  11.2 61.2 %copy-start.12 = (bf16[512,8]{0,1:T(8,128)(2,1)S(1)}, bf16[512,8]{0,1:T(8,128)(2,1)}, u32[]{:S(2)}) copy-start(bf16[512,8]{0,1:T(8,128)(2,1)} %param.27) | copy-start | bytes 24580
  11.2 1324.9 %all-gather.24.cloned.1.call-start = ((), (), s32[]{:S(2)}) async-start(), calls=%async_computation.6 | async-start | bytes 75497472 | tf_op jit(solution)/shard_map/all_gather | solution.py:98
  305.9 3.7 copy-start.18
  373.6 83.0 %copy-start.4 = (bf16[16,32,8,128]{3,2,1,0:T(8,128)(2,1)}, bf16[16,32,8,128]{3,2,1,0:T(8,128)(2,1)S(1)}, u32[]{:S(2)}) copy-start(bf16[16,32,8,128]{3,2,1,0:T(8,128)(2,1)S(1)} %get-tuple-element.232) | copy-start | bytes 3145732
  373.6 83.1 %copy-start.5 = (bf16[16,32,8,128]{3,2,1,0:T(8,128)(2,1)}, bf16[16,32,8,128]{3,2,1,0:T(8,128)(2,1)S(1)}, u32[]{:S(2)}) copy-start(bf16[16,32,8,128]{3,2,1,0:T(8,128)(2,1)S(1)} %get-tuple-element.233) | copy-start | bytes 3145732
  433.6 23.1 %copy-start.3 = (bf16[16,32,4096]{2,1,0:T(8,128)(2,1)S(1)}, bf16[16,32,4096]{2,1,0:T(8,128)(2,1)}, u32[]{:S(2)}) copy-start(bf16[16,32,4096]{2,1,0:T(8,128)(2,1)} %param.17) | copy-start | bytes 12582916
  459.5 3.7 copy-start.2
  461.2 2.0 copy-start
  463.2 6.9 copy-start.9
  463.2 7.0 copy-start.11
  470.2 17.8 %copy-start.13 = (pred[1024]{0:T(1024)(128)(4,1)S(1)}, pred[1024]{0:T(1024)(128)(4,1)}, u32[]{:S(2)}) copy-start(pred[1024]{0:T(1024)(128)(4,1)} %compare_and_fusion) | copy-start | bytes 3076
  1078.2 299.9 %copy-start.10 = (s32[1024]{0:T(1024)S(1)}, s32[1024]{0:T(1024)}, u32[]{:S(2)}) copy-start(s32[1024]{0:T(1024)} %fusion.46) | copy-start | bytes 12292
  1398.5 20.1 %copy-start.6 = (pred[512,2]{1,0:T(8,128)(4,1)S(1)}, pred[512,2]{1,0:T(8,128)(4,1)}, u32[]{:S(2)}) copy-start(pred[512,2]{1,0:T(8,128)(4,1)} %broadcast_in_dim.76) | copy-start | bytes 3076
  1418.5 41.2 %copy-start.7 = (f32[8,1,512]{2,1,0:T(1,128)S(1)}, f32[8,1,512]{2,1,0:T(1,128)}, u32[]{:S(2)}) copy-start(f32[8,1,512]{2,1,0:T(1,128)} %convert_element_type.106) | copy-start | bytes 49156
  1455.5 5.8 copy-start.1
Sparse Core Ops, SparseCore 0:
  9.8 53.4 all-gather.13
  65.2 50.7 all-gather.11
  117.8 157.0 all-gather.15
  276.5 157.0 all-gather.17
  435.3 299.0 all-gather.19
  736.1 299.0 all-gather.21
  1037.0 299.0 all-gather.23
where the time goes:
time: 1480 us; the launch traced here: 1470 us
  waiting for transfers between devices  982 us (66%)
  Pallas kernels  119 us (8%)
  other arithmetic  112 us (8%)
  local copies, waits for them, and re-layouts  107 us (7%)
  matrix products  93.7 us (6%)
  blocking collectives  44.7 us (3%)
  between operations  15 us (1%)
    all_gather x1, waiting for transfers between devices, device_fn(): gather_dim1(w_up)  263 us
    all_gather x1, waiting for transfers between devices, device_fn(): gather_dim1(w_down)  258 us
    all_gather x1, waiting for transfers between devices, device_fn(): gather_dim1(w_gate)  239 us
    all_gather x1, waiting for transfers between devices, device_fn(): q_proj = dot_f32(h_attn, gather_dim0(w_query)).astype(jnp.bfloat16)  148 us
    another operation x3, Pallas kernels  118 us
    dot_general x5, matrix products, dot_f32(): return jnp.dot(left_op, right_op, preferred_element_type=jnp.float32)  64.6 us
    all_gather x1, waiting for transfers between devices, device_fn(): attn_out = dot_f32(context_rows, gather_dim0(w_attn_out))  51.8 us
    gather x2, local copies, waits for them, and re-layouts, moe_rows(): jnp.take(expert_out, jnp.argsort(pair_order), axis=0)  40.5 us
  transfers between devices with their start and end apart: 7, of which 6 were waited for; matrix products, arithmetic and copies ran while one was open for 15% of the time, Pallas kernels for 5%

commit v1 on v0

v1 whole, which is shorter than its diff:
```python
import functools
import jax
import jax.numpy as jnp
from jax import lax
from jax.sharding import PartitionSpec as P

HEAD_DIM = 128
SOFT_CAP = 30.0
NORM_EPS = 1e-5
ROPE_BASE = 10000.0
ATTN_SCALE = HEAD_DIM ** -0.5


def dot_f32(left_op, right_op):
    return jnp.dot(left_op, right_op, preferred_element_type=jnp.float32)


def rms_norm(values, gain_vec):
    values_f32 = values.astype(jnp.float32)
    inv_rms = lax.rsqrt(jnp.mean(values_f32 * values_f32, axis=-1, keepdims=True) + NORM_EPS)
    return values_f32 * inv_rms * gain_vec.astype(jnp.float32)


def rope_tables(seq_len):
    half_dim = HEAD_DIM // 2
    inv_freq = ROPE_BASE ** (-jnp.arange(half_dim, dtype=jnp.float32) * (2.0 / HEAD_DIM))
    angles = jnp.arange(seq_len, dtype=jnp.float32)[:, None] * inv_freq[None, :]
    return jnp.cos(angles)[:, None, :], jnp.sin(angles)[:, None, :]


def apply_rope(values, cos_t, sin_t):
    half_dim = HEAD_DIM // 2
    values_f32 = values.astype(jnp.float32)
    first_half = values_f32[..., :half_dim]
    second_half = values_f32[..., half_dim:]
    return jnp.concatenate([first_half * cos_t - second_half * sin_t, second_half * cos_t + first_half * sin_t], axis=-1).astype(jnp.bfloat16)


def attend(q_groups, k_rows, v_rows, lengths):
    positions = jnp.arange(q_groups.shape[1])
    scores = jnp.einsum('bqkgd,bskd->bkgqs', q_groups, k_rows, preferred_element_type=jnp.float32) * ATTN_SCALE
    scores = SOFT_CAP * jnp.tanh(scores / SOFT_CAP)
    allowed = (positions[None, :] <= positions[:, None])[None] & (positions[None, None, :] < lengths[:, None, None])
    scores = jnp.where(allowed[:, None, None], scores, -1e30)
    attn_probs = jax.nn.softmax(scores, axis=-1).astype(jnp.bfloat16)
    return jnp.einsum('bkgqs,bskd->bqkgd', attn_probs, v_rows, preferred_element_type=jnp.float32).astype(jnp.bfloat16)


def solution(mesh):
    row_spec = P(('dp', 'wg'))
    dim0_spec = P('wg', None)
    dim1_spec = P(None, 'wg', None)

    def half_gather(shard, axis):
        n = shard.shape[axis] // 2
        part = lax.dynamic_slice_in_dim(shard, lax.axis_index('dp') * n, n, axis=axis)
        return lax.all_gather(part, ('wg', 'dp'), axis=axis, tiled=True)

    def device_fn(hidden, seq_lens, route_idx, g_attn_in, w_query, w_key, w_value, w_attn_out, g_attn_out, g_moe_in, w_router, w_gate, w_up, w_down, g_moe_out):
        n_prompts, seq_len, d_model = hidden.shape
        n_exp = w_gate.shape[0]
        n_wg = lax.axis_size('wg')
        small = jnp.concatenate([g_attn_in[None], g_attn_out[None], g_moe_in[None], g_moe_out[None], w_router.T], axis=0)
        small = lax.all_gather(small, 'wg', axis=0)
        small = small.transpose(1, 0, 2).reshape(4 + n_exp, d_model)
        tok_rows = hidden.reshape(n_prompts * seq_len, d_model)
        h_attn = rms_norm(tok_rows, small[0]).astype(jnp.bfloat16)
        k_proj = dot_f32(h_attn, half_gather(w_key, 0)).astype(jnp.bfloat16)
        v_proj = dot_f32(h_attn, half_gather(w_value, 0)).astype(jnp.bfloat16)
        q_proj = dot_f32(h_attn, half_gather(w_query, 0)).astype(jnp.bfloat16)
        n_heads = q_proj.shape[1] // HEAD_DIM
        n_kv = k_proj.shape[1] // HEAD_DIM
        cos_t, sin_t = rope_tables(seq_len)
        q_rope = apply_rope(q_proj.reshape(n_prompts, seq_len, n_heads, HEAD_DIM), cos_t, sin_t)
        k_rope = apply_rope(k_proj.reshape(n_prompts, seq_len, n_kv, HEAD_DIM), cos_t, sin_t)
        v_heads = v_proj.reshape(n_prompts, seq_len, n_kv, HEAD_DIM)
        q_groups = q_rope.reshape(n_prompts, seq_len, n_kv, n_heads // n_kv, HEAD_DIM)
        context = attend(q_groups, k_rope, v_heads, seq_lens).reshape(n_prompts * seq_len, n_heads * HEAD_DIM)
        attn_out = dot_f32(context, half_gather(w_attn_out, 0))
        mid_rows = (tok_rows.astype(jnp.float32) + rms_norm(attn_out, small[1])).astype(jnp.bfloat16)
        h_moe = rms_norm(mid_rows, small[2]).astype(jnp.bfloat16)
        router_probs = jax.nn.softmax(lax.dot_general(h_moe, small[4:], (((1,), (1,)), ((), ())), preferred_element_type=jnp.float32), axis=-1)
        exp_ids = jnp.arange(n_exp)
        chosen = (route_idx[:, :, None] == exp_ids).any(axis=1)
        combine = jnp.where(chosen, router_probs, 0.0)
        moe_out = jnp.zeros((n_prompts * seq_len, d_model), jnp.float32)
        step = 2
        for e0 in range(0, n_exp, step):
            wg_ = half_gather(w_gate[e0:e0 + step], 1)
            wu_ = half_gather(w_up[e0:e0 + step], 1)
            wd_ = half_gather(w_down[e0:e0 + step], 1)
            for i in range(step):
                act = (jax.nn.gelu(dot_f32(h_moe, wg_[i])) * dot_f32(h_moe, wu_[i])).astype(jnp.bfloat16)
                moe_out = moe_out + combine[:, e0 + i][:, None] * dot_f32(act, wd_[i])
        y_rows = (mid_rows.astype(jnp.float32) + rms_norm(moe_out, small[3])).astype(jnp.bfloat16)
        return y_rows.reshape(hidden.shape), k_rope, v_heads

    return jax.shard_map(
        device_fn,
        mesh=mesh,
        in_specs=(row_spec, row_spec, row_spec, P('wg'), dim0_spec, dim0_spec, dim0_spec, dim0_spec, P('wg'), P('wg'), dim0_spec, dim1_spec, dim1_spec, dim1_spec, P('wg')),
        out_specs=(row_spec, row_spec, row_spec),
        check_vma=False,
    )
```

time: 1480 us -> 1390 us (0.939)
  matrix products: 93.7 us -> 321 us
  Pallas kernels: 119 us -> 0 us
  other arithmetic: 112 us -> 30.3 us
  waiting for transfers between devices: 982 us -> 930 us
  blocking collectives: 44.7 us -> 10.9 us
  local copies, waits for them, and re-layouts: 107 us -> 77.1 us
    dot_general x5 -> x21, matrix products: 64.6 us -> 311 us  [dot_f32(): return jnp.dot(left_op, right_op, preferred_element_type=jnp.float32)]
    another operation x3 -> x0, Pallas kernels: 118 us -> none
    gather x8 -> x0, local copies, waits for them, and re-layouts: 65.4 us -> none  [the longest x2 40.5 us: moe_rows(): jnp.take(expert_out, jnp.argsort(pair_order), axis=0)]
    all_gather x7 -> x16, waiting for transfers between devices: 978 us -> 929 us  [half_gather(): return lax.all_gather(part, ('wg', 'dp'), axis=axis, tiled=True)]
    reduce_sum x2 -> x1, other arithmetic: 37 us -> 0.02 us  [device_fn(): jax.nn.softmax(lax.dot_general(h_moe, small[4:], (((1,), (1,)), ((), ()))...]
    all_gather x5 -> x1, blocking collectives: 44.7 us -> 10.9 us  [device_fn(): small = lax.all_gather(small, 'wg', axis=0)]
    sub x16 -> x0, matrix products: 24.5 us -> none  [attend_prompt(): attn_probs = jax.nn.softmax(scores, axis=-1).astype(jnp.bfloat16)]
    dynamic_slice x32 -> x16, local copies, waits for them, and re-layouts: 9.57 us -> 30.5 us  [half_gather(): lax.dynamic_slice_in_dim(shard, lax.axis_index('dp') * n, n, axis=axis)]
  transfers between devices with their start and end apart: 7 -> 16, of which waited for: 6 -> 15; matrix products, arithmetic and copies ran while one was open for 15% -> 26% of each run, Pallas kernels for 5% -> 0%
where the time goes in v1:
time: 1390 us; the launch traced here: 1380 us
  waiting for transfers between devices  930 us (67%)
  matrix products  321 us (23%)
  local copies, waits for them, and re-layouts  77.1 us (6%)
  other arithmetic  30.3 us (2%)
  between operations  14.7 us (1%)
    all_gather x16, waiting for transfers between devices, half_gather(): return lax.all_gather(part, ('wg', 'dp'), axis=axis, tiled=True)  929 us
    dot_general x21, matrix products, dot_f32(): return jnp.dot(left_op, right_op, preferred_element_type=jnp.float32)  311 us
    dynamic_slice x16, local copies, waits for them, and re-layouts, half_gather(): lax.dynamic_slice_in_dim(shard, lax.axis_index('dp') * n, n, axis=axis)  30.5 us
  transfers between devices with their start and end apart: 16, of which 15 were waited for; matrix products, arithmetic and copies ran while one was open for 26% of the time, Pallas kernels for 0%

profile of v1, /device:TPU:0, one launch (start us, length us, event | category | flops | bytes accessed | tf_op | source)
XLA Modules:
  0.0 1383.9 jit_solution(15872184295727227187)
XLA Ops:
  11.2 3.2 constant_dynamic-slice_fusion.13
  14.5 3.1 constant_dynamic-slice_fusion.12
  17.7 5.2 fusion.209
  29.9 5.4 fusion.208
  36.4 5.7 fusion.210
  56.7 10.9 all-gather.1
  71.6 5.8 fusion.31
  77.7 8.6 convert_bitcast_fusion.2
  88.8 25.0 %all-gather.19.cloned.1.call-done = bf16[4096,1024]{1,0:T(8,128)(2,1)} async-done(((bf16[256,1024]{1,0:T(8,128)(2,1)}), bf16[4096,1024]{1,0:T(8,128)(2,1)}) %all-gather.19.cloned.1.call-update) | async-done | bytes 8388624 | tf_op jit(solution)/shard_map/all_gather | solution.py:57
  113.8 9.3 fusion.115
  127.3 120.0 %all-gather.23.cloned.1.call-done = bf16[4096,4096]{1,0:T(8,128)(2,1)} async-done(((bf16[256,4096]{1,0:T(8,128)(2,1)}), bf16[4096,4096]{1,0:T(8,128)(2,1)}) %all-gather.23.cloned.1.call-update) | async-done | bytes 33554448 | tf_op jit(solution)/shard_map/all_gather | solution.py:57
  247.3 22.8 %convert_bitcast_fusion = f32[64,8,32,128]{3,1,2,0:T(8,128)S(1)} fusion(bf16[512,4096]{1,0:T(8,128)(2,1)} %fusion.31, bf16[4096,4096]{1,0:T(8,128)(2,1)} %all-gather.23.cloned.1.call-done), kind=kOutput, calls=%fused_computation.64 | convolution fusion | flops 17184063488 | bytes 46137344 | tf_op jit(solution)/shard_map/dot_general | solution.py:15
  278.6 7.0 fusion.34
  285.6 4.1 fusion.213
  291.6 4.2 copy.50
  295.8 7.8 reshape.194
  303.6 77.2 %all-gather.25.cloned.1.call-done = bf16[4096,4096]{1,0:T(8,128)(2,1)} async-done(((bf16[256,4096]{1,0:T(8,128)(2,1)}), bf16[4096,4096]{1,0:T(8,128)(2,1)}) %all-gather.25.cloned.1.call-update) | async-done | bytes 33554448 | tf_op jit(solution)/shard_map/all_gather | solution.py:57
  380.7 23.0 %multiply_reduce_fusion.1 = (f32[512]{0:T(512)S(1)}, f32[512,4096]{1,0:T(8,128)S(1)}) fusion(bf16[512,4096]{1,0:T(8,128)(2,1)} %reshape.194, bf16[4096,4096]{1,0:T(8,128)(2,1)} %all-gather.25.cloned.1.call-done), kind=kOutput, calls=%fused_computation.67 | convolution fusion | flops 17184063488 | bytes 46139392 | tf_op jit(solution)/shard_map/dot_general | solution.py:15
  410.8 48.1 %all-gather.45.cloned.1.call-done = bf16[2,4096,1024]{2,1,0:T(8,128)(2,1)} async-done(((bf16[2,256,1024]{2,1,0:T(8,128)(2,1)}), bf16[2,4096,1024]{2,1,0:T(8,128)(2,1)}) %all-gather.45.cloned.1.call-update) | async-done | bytes 16777232 | tf_op jit(solution)/shard_map/all_gather | solution.py:57
  458.9 10.7 fusion.7
  470.3 5.9 fusion.10
  476.3 60.8 %all-gather.39.cloned.1.call-done = bf16[2,4096,1024]{2,1,0:T(8,128)(2,1)} async-done(((bf16[2,256,1024]{2,1,0:T(8,128)(2,1)}), bf16[2,4096,1024]{2,1,0:T(8,128)(2,1)}) %all-gather.39.cloned.1.call-update) | async-done | bytes 16777232 | tf_op jit(solution)/shard_map/all_gather | solution.py:57
  537.1 10.7 fusion.13
  548.5 6.2 fusion.16
  554.7 60.7 %all-gather.33.cloned.1.call-done = bf16[2,4096,1024]{2,1,0:T(8,128)(2,1)} async-done(((bf16[2,256,1024]{2,1,0:T(8,128)(2,1)}), bf16[2,4096,1024]{2,1,0:T(8,128)(2,1)}) %all-gather.33.cloned.1.call-update) | async-done | bytes 16777232 | tf_op jit(solution)/shard_map/all_gather | solution.py:57
  615.4 9.3 fusion.19
  626.1 5.9 fusion.22
  632.0 61.7 %all-gather.27.cloned.1.call-done = bf16[2,4096,1024]{2,1,0:T(8,128)(2,1)} async-done(((bf16[2,256,1024]{2,1,0:T(8,128)(2,1)}), bf16[2,4096,1024]{2,1,0:T(8,128)(2,1)}) %all-gather.27.cloned.1.call-update) | async-done | bytes 16777232 | tf_op jit(solution)/shard_map/all_gather | solution.py:57
  693.7 10.7 fusion.25
  705.1 5.9 fusion.28
  711.0 61.0 %all-gather.29.cloned.1.call-done = bf16[2,4096,1024]{2,1,0:T(8,128)(2,1)} async-done(((bf16[2,256,1024]{2,1,0:T(8,128)(2,1)}), bf16[2,4096,1024]{2,1,0:T(8,128)(2,1)}) %all-gather.29.cloned.1.call-update) | async-done | bytes 16777232 | tf_op jit(solution)/shard_map/all_gather | solution.py:57
  772.0 11.4 fusion.51
  783.4 66.7 %all-gather.49.cloned.1.call-done = bf16[2,1024,4096]{2,1,0:T(8,128)(2,1)} async-done(((bf16[2,64,4096]{2,1,0:T(8,128)(2,1)}), bf16[2,1024,4096]{2,1,0:T(8,128)(2,1)}) %all-gather.49.cloned.1.call-update) | async-done | bytes 16777232 | tf_op jit(solution)/shard_map/all_gather | solution.py:57
  850.2 78.3 %all-gather.47.cloned.1.call-done = bf16[2,4096,1024]{2,1,0:T(8,128)(2,1)} async-done(((bf16[2,256,1024]{2,1,0:T(8,128)(2,1)}), bf16[2,4096,1024]{2,1,0:T(8,128)(2,1)}) %all-gather.47.cloned.1.call-update) | async-done | bytes 16777232 | tf_op jit(solution)/shard_map/all_gather | solution.py:57
  928.5 20.1 %fusion.5 = f32[512,4096]{1,0:T(8,128)} fusion(bf16[2,1024,4096]{2,1,0:T(8,128)(2,1)} %all-gather.49.cloned.1.call-done, f32[512,1024]{1,0:T(8,128)} %fusion.7, bf16[2,4096,1024]{2,1,0:T(8,128)(2,1)} %all-gather.47.cloned.1.call-done, bf16[512,4096]{1,0:T(8,128)(2,1)} %copy-done.3, f32[4096]{0:T(1024)S(1)} %bitcast.209, f32[512]{0:T(512)S(1)} %add_rsqrt_fusion.2), kind=kOutput, calls=%fused_computation.9 | convolution fusion | flops 8603566080 | bytes 31475712 | tf_op jit(solution)/shard_map/dot_general | solution.py:15
  948.6 20.2 %fusion.8 = f32[512,4096]{1,0:T(8,128)} fusion(bf16[2,1024,4096]{2,1,0:T(8,128)(2,1)} %all-gather.49.cloned.1.call-done, f32[512,1024]{1,0:T(8,128)} %fusion.10, bf16[2,4096,1024]{2,1,0:T(8,128)(2,1)} %all-gather.47.cloned.1.call-done, bf16[512,4096]{1,0:T(8,128)(2,1)} %copy-done.3, f32[4096]{0:T(1024)S(1)} %bitcast.210, f32[512]{0:T(512)S(1)} %add_rsqrt_fusion.2), kind=kOutput, calls=%fused_computation.15 | convolution fusion | flops 8603566080 | bytes 31475712 | tf_op jit(solution)/shard_map/dot_general | solution.py:15
  968.8 37.8 %all-gather.43.cloned.1.call-done = bf16[2,1024,4096]{2,1,0:T(8,128)(2,1)} async-done(((bf16[2,64,4096]{2,1,0:T(8,128)(2,1)}), bf16[2,1024,4096]{2,1,0:T(8,128)(2,1)}) %all-gather.43.cloned.1.call-update) | async-done | bytes 16777232 | tf_op jit(solution)/shard_map/all_gather | solution.py:57
  1006.7 78.3 %all-gather.41.cloned.1.call-done = bf16[2,4096,1024]{2,1,0:T(8,128)(2,1)} async-done(((bf16[2,256,1024]{2,1,0:T(8,128)(2,1)}), bf16[2,4096,1024]{2,1,0:T(8,128)(2,1)}) %all-gather.41.cloned.1.call-update) | async-done | bytes 16777232 | tf_op jit(solution)/shard_map/all_gather | solution.py:57
  1085.0 20.1 %fusion.11 = f32[512,4096]{1,0:T(8,128)} fusion(bf16[2,1024,4096]{2,1,0:T(8,128)(2,1)} %all-gather.43.cloned.1.call-done, f32[512,1024]{1,0:T(8,128)} %fusion.13, bf16[2,4096,1024]{2,1,0:T(8,128)(2,1)} %all-gather.41.cloned.1.call-done, bf16[512,4096]{1,0:T(8,128)(2,1)} %copy-done.3, f32[4096]{0:T(1024)S(1)} %bitcast.211, f32[512]{0:T(512)S(1)} %add_rsqrt_fusion.2), kind=kOutput, calls=%fused_computation.21 | convolution fusion | flops 8603566080 | bytes 31475712 | tf_op jit(solution)/shard_map/dot_general | solution.py:15
  1105.1 20.8 %fusion.14 = f32[512,4096]{1,0:T(8,128)} fusion(bf16[2,1024,4096]{2,1,0:T(8,128)(2,1)} %all-gather.43.cloned.1.call-done, f32[512,1024]{1,0:T(8,128)} %fusion.16, bf16[2,4096,1024]{2,1,0:T(8,128)(2,1)} %all-gather.41.cloned.1.call-done, bf16[512,4096]{1,0:T(8,128)(2,1)} %copy-done.3, f32[4096]{0:T(1024)S(1)} %bitcast.212, f32[512]{0:T(512)S(1)} %add_rsqrt_fusion.2), kind=kOutput, calls=%fused_computation.27 | convolution fusion | flops 8603566080 | bytes 31475712 | tf_op jit(solution)/shard_map/dot_general | solution.py:15
  1125.8 37.3 %all-gather.37.cloned.1.call-done = bf16[2,1024,4096]{2,1,0:T(8,128)(2,1)} async-done(((bf16[2,64,4096]{2,1,0:T(8,128)(2,1)}), bf16[2,1024,4096]{2,1,0:T(8,128)(2,1)}) %all-gather.37.cloned.1.call-update) | async-done | bytes 16777232 | tf_op jit(solution)/shard_map/all_gather | solution.py:57
  1163.2 78.2 %all-gather.35.cloned.1.call-done = bf16[2,4096,1024]{2,1,0:T(8,128)(2,1)} async-done(((bf16[2,256,1024]{2,1,0:T(8,128)(2,1)}), bf16[2,4096,1024]{2,1,0:T(8,128)(2,1)}) %all-gather.35.cloned.1.call-update) | async-done | bytes 16777232 | tf_op jit(solution)/shard_map/all_gather | solution.py:57
  1241.3 19.5 %fusion.17 = f32[512,4096]{1,0:T(8,128)} fusion(bf16[2,1024,4096]{2,1,0:T(8,128)(2,1)} %all-gather.37.cloned.1.call-done, f32[512,1024]{1,0:T(8,128)S(1)} %fusion.19, bf16[2,4096,1024]{2,1,0:T(8,128)(2,1)} %all-gather.35.cloned.1.call-done, bf16[512,4096]{1,0:T(8,128)(2,1)} %copy-done.3, f32[4096]{0:T(1024)S(1)} %bitcast.213, f32[512]{0:T(512)S(1)} %add_rsqrt_fusion.2), kind=kOutput, calls=%fused_computation.33 | convolution fusion | flops 8603566080 | bytes 31475712 | tf_op jit(solution)/shard_map/dot_general | solution.py:15
  1260.8 20.5 %fusion.20 = f32[512,4096]{1,0:T(8,128)} fusion(bf16[2,1024,4096]{2,1,0:T(8,128)(2,1)} %all-gather.37.cloned.1.call-done, f32[512,1024]{1,0:T(8,128)} %fusion.22, bf16[2,4096,1024]{2,1,0:T(8,128)(2,1)} %all-gather.35.cloned.1.call-done, bf16[512,4096]{1,0:T(8,128)(2,1)} %copy-done.3, f32[4096]{0:T(1024)S(1)} %bitcast.214, f32[512]{0:T(512)S(1)} %add_rsqrt_fusion.2), kind=kOutput, calls=%fused_computation.39 | convolution fusion | flops 8603566080 | bytes 31475712 | tf_op jit(solution)/shard_map/dot_general | solution.py:15
  1281.4 38.1 %all-gather.31.cloned.1.call-done = bf16[2,1024,4096]{2,1,0:T(8,128)(2,1)} async-done(((bf16[2,64,4096]{2,1,0:T(8,128)(2,1)}), bf16[2,1024,4096]{2,1,0:T(8,128)(2,1)}) %all-gather.31.cloned.1.call-update) | async-done | bytes 16777232 | tf_op jit(solution)/shard_map/all_gather | solution.py:57
  1319.5 19.7 %fusion.23 = f32[512,4096]{1,0:T(8,128)} fusion(bf16[2,1024,4096]{2,1,0:T(8,128)(2,1)} %all-gather.31.cloned.1.call-done, f32[512,1024]{1,0:T(8,128)S(1)} %copy-done.31, bf16[2,4096,1024]{2,1,0:T(8,128)(2,1)} %all-gather.29.cloned.1.call-done, bf16[512,4096]{1,0:T(8,128)(2,1)} %copy-done.3, f32[4096]{0:T(1024)S(1)} %bitcast.215, f32[512]{0:T(512)S(1)} %add_rsqrt_fusion.2), kind=kOutput, calls=%fused_computation.45 | convolution fusion | flops 8603566080 | bytes 31475712 | tf_op jit(solution)/shard_map/dot_general | solution.py:15
  1339.3 29.2 %multiply_reduce_fusion = (f32[512]{0:T(512)S(1)}, f32[512,4096]{1,0:T(8,128)}) fusion(f32[512,4096]{1,0:T(8,128)} %fusion.5, f32[512]{0:T(512)S(1)} %bitcast.192, f32[512,4096]{1,0:T(8,128)} %fusion.8, f32[512]{0:T(512)S(1)} %bitcast.193, f32[512,4096]{1,0:T(8,128)} %fusion.11, f32[512]{0:T(512)S(1)} %bitcast.194, f32[512,4096]{1,0:T(8,128)} %fusion.14, ...), kind=kOutput, calls=%fused_computation.65 | convolution fusion | flops 4330618368 | bytes 76564480 | tf_op jit(solution)/shard_map/dot_general | solution.py:15
  1368.5 8.7 fusion.4
  (146 shorter events, 58.4 us)
Async XLA Ops:
  7.2 1.2 copy-start
  7.2 70.5 %all-gather.21.cloned.1.call-start = ((), (), s32[]{:S(2)}) async-start(), calls=%async_computation.1 | async-start | bytes 8912896 | tf_op jit(solution)/shard_map/all_gather | solution.py:57
  9.2 104.5 %all-gather.19.cloned.1.call-start = ((), (), s32[]{:S(2)}) async-start(), calls=%async_computation | async-start | bytes 8912896 | tf_op jit(solution)/shard_map/all_gather | solution.py:57
  11.2 236.1 %all-gather.23.cloned.1.call-start = ((), (), s32[]{:S(2)}) async-start(), calls=%async_computation.2 | async-start | bytes 35651584 | tf_op jit(solution)/shard_map/all_gather | solution.py:57
  14.4 366.3 %all-gather.25.cloned.1.call-start = ((), (), s32[]{:S(2)}) async-start(), calls=%async_computation.3 | async-start | bytes 35651584 | tf_op jit(solution)/shard_map/all_gather | solution.py:57
  17.7 441.2 %all-gather.45.cloned.1.call-start = ((), (), s32[]{:S(2)}) async-start(), calls=%async_computation.13 | async-start | bytes 17825792 | tf_op jit(solution)/shard_map/all_gather | solution.py:57
  24.0 513.1 %all-gather.39.cloned.1.call-start = ((), (), s32[]{:S(2)}) async-start(), calls=%async_computation.10 | async-start | bytes 17825792 | tf_op jit(solution)/shard_map/all_gather | solution.py:57
  26.4 589.0 %all-gather.33.cloned.1.call-start = ((), (), s32[]{:S(2)}) async-start(), calls=%async_computation.7 | async-start | bytes 17825792 | tf_op jit(solution)/shard_map/all_gather | solution.py:57
  28.7 665.0 %all-gather.27.cloned.1.call-start = ((), (), s32[]{:S(2)}) async-start(), calls=%async_computation.4 | async-start | bytes 17825792 | tf_op jit(solution)/shard_map/all_gather | solution.py:57
  29.9 742.2 %all-gather.29.cloned.1.call-start = ((), (), s32[]{:S(2)}) async-start(), calls=%async_computation.5 | async-start | bytes 17825792 | tf_op jit(solution)/shard_map/all_gather | solution.py:57
  36.4 813.8 %all-gather.49.cloned.1.call-start = ((), (), s32[]{:S(2)}) async-start(), calls=%async_computation.15 | async-start | bytes 17825792 | tf_op jit(solution)/shard_map/all_gather | solution.py:57
  43.3 885.2 %all-gather.47.cloned.1.call-start = ((), (), s32[]{:S(2)}) async-start(), calls=%async_computation.14 | async-start | bytes 17825792 | tf_op jit(solution)/shard_map/all_gather | solution.py:57
  45.6 10.8 copy-start.22
  45.6 10.9 copy-start.23
  45.6 10.9 copy-start.24
  45.6 10.9 copy-start.25
  45.6 10.9 copy-start.20
  45.7 961.0 %all-gather.43.cloned.1.call-start = ((), (), s32[]{:S(2)}) async-start(), calls=%async_computation.12 | async-start | bytes 17825792 | tf_op jit(solution)/shard_map/all_gather | solution.py:57
  48.1 1036.9 %all-gather.41.cloned.1.call-start = ((), (), s32[]{:S(2)}) async-start(), calls=%async_computation.11 | async-start | bytes 17825792 | tf_op jit(solution)/shard_map/all_gather | solution.py:57
  48.1 23.4 %copy-start.26 = (s32[16]{0:T(128)S(1)}, s32[16]{0:T(128)}, u32[]{:S(2)}) copy-start(s32[16]{0:T(128)} %param.16) | copy-start | bytes 196
  48.1 23.5 %copy-start.21 = (s32[512,2]{0,1:T(2,128)S(1)}, s32[512,2]{0,1:T(2,128)}, u32[]{:S(2)}) copy-start(s32[512,2]{0,1:T(2,128)} %param.17) | copy-start | bytes 12292
  50.4 1112.7 %all-gather.37.cloned.1.call-start = ((), (), s32[]{:S(2)}) async-start(), calls=%async_computation.9 | async-start | bytes 17825792 | tf_op jit(solution)/shard_map/all_gather | solution.py:57
  52.8 1188.5 %all-gather.35.cloned.1.call-start = ((), (), s32[]{:S(2)}) async-start(), calls=%async_computation.8 | async-start | bytes 17825792 | tf_op jit(solution)/shard_map/all_gather | solution.py:57
  54.0 1265.5 %all-gather.31.cloned.1.call-start = ((), (), s32[]{:S(2)}) async-start(), calls=%async_computation.6 | async-start | bytes 17825792 | tf_op jit(solution)/shard_map/all_gather | solution.py:57
  113.8 10.5 copy-start.8
  285.5 4.1 copy-start.10
  380.7 23.1 %copy-start.2 = (bf16[16,32,4096]{2,1,0:T(8,128)(2,1)S(1)}, bf16[16,32,4096]{2,1,0:T(8,128)(2,1)}, u32[]{:S(2)}) copy-start(bf16[16,32,4096]{2,1,0:T(8,128)(2,1)} %param.15) | copy-start | bytes 12582916
  406.7 2.0 copy-start.3
  458.9 10.8 copy-start.4
  458.9 11.5 copy-start.27
  537.1 10.7 copy-start.5
  537.1 11.5 copy-start.28
  615.4 9.3 copy-start.6
  615.4 10.7 copy-start.29
  693.7 10.7 copy-start.7
  693.7 11.5 copy-start.30
  1260.8 58.7 %copy-start.31 = (f32[512,1024]{1,0:T(8,128)S(1)}, f32[512,1024]{1,0:T(8,128)}, u32[]{:S(2)}) copy-start(f32[512,1024]{1,0:T(8,128)} %fusion.25) | copy-start | bytes 6291460
  1281.3 57.9 %copy-start.9 = (bf16[512,1024]{1,0:T(8,128)(2,1)S(1)}, bf16[512,1024]{1,0:T(8,128)(2,1)}, u32[]{:S(2)}) copy-start(bf16[512,1024]{1,0:T(8,128)(2,1)} %fusion.51) | copy-start | bytes 3145732
  1281.3 57.9 %copy-start.12 = (f32[512,1]{0,1:T(1,128)S(1)}, f32[512,1]{0,1:T(1,128)}, u32[]{:S(2)}) copy-start(f32[512,1]{0,1:T(1,128)} %get-tuple-element.39) | copy-start | bytes 6148
  1281.3 57.9 %copy-start.13 = (f32[512,1]{0,1:T(1,128)S(1)}, f32[512,1]{0,1:T(1,128)}, u32[]{:S(2)}) copy-start(f32[512,1]{0,1:T(1,128)} %get-tuple-element.40) | copy-start | bytes 6148
  1281.3 57.9 %copy-start.14 = (f32[512,1]{0,1:T(1,128)S(1)}, f32[512,1]{0,1:T(1,128)}, u32[]{:S(2)}) copy-start(f32[512,1]{0,1:T(1,128)} %get-tuple-element.41) | copy-start | bytes 6148
  1281.4 57.9 %copy-start.15 = (f32[512,1]{0,1:T(1,128)S(1)}, f32[512,1]{0,1:T(1,128)}, u32[]{:S(2)}) copy-start(f32[512,1]{0,1:T(1,128)} %get-tuple-element.42) | copy-start | bytes 6148
  1281.4 57.9 %copy-start.16 = (f32[512,1]{0,1:T(1,128)S(1)}, f32[512,1]{0,1:T(1,128)}, u32[]{:S(2)}) copy-start(f32[512,1]{0,1:T(1,128)} %get-tuple-element.43) | copy-start | bytes 6148
  1281.4 57.9 %copy-start.17 = (f32[512,1]{0,1:T(1,128)S(1)}, f32[512,1]{0,1:T(1,128)}, u32[]{:S(2)}) copy-start(f32[512,1]{0,1:T(1,128)} %get-tuple-element.44) | copy-start | bytes 6148
  1281.4 57.9 %copy-start.18 = (f32[512,1]{0,1:T(1,128)S(1)}, f32[512,1]{0,1:T(1,128)}, u32[]{:S(2)}) copy-start(f32[512,1]{0,1:T(1,128)} %get-tuple-element.45) | copy-start | bytes 6148
  1281.4 57.9 %copy-start.19 = (f32[512,1]{0,1:T(1,128)S(1)}, f32[512,1]{0,1:T(1,128)}, u32[]{:S(2)}) copy-start(f32[512,1]{0,1:T(1,128)} %get-tuple-element.46) | copy-start | bytes 6148
  1339.3 29.2 %copy-start.11 = (f32[1,8,512]{2,0,1:T(1,128)S(1)}, f32[1,8,512]{2,0,1:T(1,128)}, u32[]{:S(2)}) copy-start(f32[1,8,512]{2,0,1:T(1,128)} %get-tuple-element.35) | copy-start | bytes 49156
  1368.5 8.7 copy-start.1
Sparse Core Ops, SparseCore 0:
  10.8 51.4 all-gather.20
  65.1 48.6 all-gather.18
  116.0 131.2 all-gather.22
  249.4 131.2 all-gather.24
  382.8 76.0 all-gather.44
  461.0 76.0 all-gather.38
  539.3 76.0 all-gather.32
  617.6 76.0 all-gather.26
  696.0 76.0 all-gather.28
  774.1 76.0 all-gather.48
  852.5 76.0 all-gather.46
  930.6 76.0 all-gather.42
  1008.9 76.0 all-gather.40
  1087.1 76.0 all-gather.36
  1165.3 76.0 all-gather.34
  1243.4 76.0 all-gather.30

commit v2 on v1

v2 whole, which is shorter than its diff:
```python
import functools
import jax
import jax.numpy as jnp
import numpy as np
from jax import lax
from jax.experimental import pallas as pl
from jax.experimental.pallas import tpu as pltpu
from jax.sharding import PartitionSpec as P

HEAD_DIM = 128
SOFT_CAP = 30.0
NORM_EPS = 1e-5
ROPE_BASE = 10000.0
ATTN_SCALE = HEAD_DIM ** -0.5
MESH_ID = pl.DeviceIdType.MESH
F32 = jnp.float32
BF16 = jnp.bfloat16

N_ROWS = 512
D_MODEL = 4096
COLS = 1024
HALF = 512
N_EXP = 8
N_DEV = 8
FRONT = 10
DOWN = FRONT + N_EXP
UNITS = DOWN + N_EXP
COPIES = 11
SLOTS = 18
HALVES = 8
LAST = UNITS - 1
SOON = 10
LOOK = 2
LAG = 2
EARLY = FRONT + 5
THEIRS = EARLY + N_EXP
LATE = THEIRS + 3


def rope_tables(seq_len, n_rows):
    half_dim = HEAD_DIM // 2
    inv_freq = (ROPE_BASE ** (-np.arange(half_dim, dtype=np.float64) * (2.0 / HEAD_DIM))).astype(np.float32)
    angles = (np.arange(n_rows) % seq_len).astype(np.float32)[:, None] * inv_freq[None, :]
    cos_t, sin_t = np.cos(angles.astype(np.float64)), np.sin(angles.astype(np.float64))
    return (np.concatenate([cos_t, cos_t], axis=1).astype(np.float32), np.concatenate([-sin_t, sin_t], axis=1).astype(np.float32))


def steps_of(s, pairs):
    value = jnp.int32(pairs[0][1])
    for start, other in pairs[1:]:
        value = jnp.where(s >= start, other, value)
    return value


def unit_at(s):
    return s + steps_of(s, ((0, 0), (4, 6), (5, -1), (9, 2), (10, -2), (12, 0), (LAST, -1)))


def tasks_done(s):
    s = jnp.asarray(s, jnp.int32)
    return steps_of(s, tuple(enumerate((0, 0, 0, 1, 2, 3, 4, 4, 5, 6, 7, 8, 9, 10, 13, 14, 16, 19, 21, 24, 25, 26, 28, 30, 31, 32, 33, 34))))


def stage_d_done(s):
    s = jnp.asarray(s, jnp.int32)
    count = jnp.where(s > SOON, s, jnp.maximum(s - 1, 0))
    return jnp.where(s >= LAST - 1, LAST, count)


def layer_kernel(x_hbm, gains_ref, router_ref, cos_ref, sin_ref, route_ref, lens_ref, wq_ref, wk_ref, wv_ref, wo_ref, wg_ref, wu_ref, wd_ref,
                 y_ref, k_ref, v_ref, ga_ref, gb_ref,
                 h_buf, o_buf, acc, w_a, w_b, res, u_buf, q_buf, u_mine, u_theirs, x_ref, gains, router, comb, mask, route_all,
                 send_sem, recv_sem, load_sem, ssend_sem, srecv_sem, zsend_sem, zrecv_sem):
    me = lax.axis_index('wg')
    z = lax.axis_index('dp')
    core = lax.rem(me, 2)
    x = lax.rem(lax.div(me, 2), 2)
    y = lax.div(me, 4)
    x_id = me + 2 - 4 * x
    y_id = me + 4 - 8 * y
    d_id = x_id + 4 - 8 * y
    p_id = me + 1 - 2 * core
    nbr_x, nbr_y, nbr_z, nbr_p = (z, x_id), (z, y_id), (1 - z, me), (z, p_id)

    x_load = pltpu.make_async_copy(x_hbm, x_ref, load_sem.at[0])
    x_load.start()
    barrier = pltpu.get_barrier_semaphore()
    for step in range(1, N_DEV):
        pl.semaphore_signal(barrier, inc=1, device_id=(z, lax.rem(me + step, N_DEV)), device_id_type=MESH_ID)
    pl.semaphore_signal(barrier, inc=1, device_id=nbr_z, device_id_type=MESH_ID)
    pl.semaphore_wait(barrier, N_DEV)

    def rows_of(owner, first, count, quarter):
        return pl.ds(pl.multiple_of(4 * quarter * owner + first * quarter, quarter), count * quarter)

    def copy(u, k, src, dst, device):
        slot = lax.rem(u, SLOTS)
        return pltpu.make_async_remote_copy(src_ref=src, dst_ref=dst, send_sem=send_sem.at[slot, k], recv_sem=recv_sem.at[slot, k],
                                            device_id=device, device_id_type=MESH_ID)

    d_first = 2 * (1 - z)
    d_other = 2 * z
    halves = (d_first, 2, d_first, d_other, 2)
    thirds = (1 - z, 3, 3 * (1 - z), 3 * z, 1)
    whole = (0, 4)

    my_half = pl.ds(pl.multiple_of(HALF * z, HALF), HALF)
    left, right = pl.ds(0, HALF), pl.ds(HALF, HALF)

    def views(u):
        return ((u < HALVES, ga_ref.at[u], 128, halves), ((u >= HALVES) & (u < FRONT), ga_ref.at[u], 128, thirds),
                ((u >= DOWN) & (u < LAST), gb_ref.at[u - DOWN], 32, thirds))

    def flat_views(u):
        return (is_pair(u), ga_ref.at[u], 128), (u == LAST, gb_ref.at[u - DOWN], 32)

    def is_pair(u):
        return (u >= FRONT) & (u < DOWN)

    def src_views(u):
        def cols(first):
            return pl.ds(pl.multiple_of((u - first) * COLS, COLS), COLS)

        return (
            (u == 0, wk_ref.at[:, :], ga_ref.at[u], 128, halves),
            (u == 1, wv_ref.at[:, :], ga_ref.at[u], 128, halves),
            ((u >= 2) & (u < 6), wq_ref.at[:, cols(2)], ga_ref.at[u], 128, halves),
            ((u >= 6) & (u < HALVES), wo_ref.at[:, cols(6)], ga_ref.at[u], 128, halves),
            ((u >= HALVES) & (u < FRONT), wo_ref.at[:, cols(6)], ga_ref.at[u], 128, thirds),
            ((u >= DOWN) & (u < LAST), wd_ref.at[u - DOWN], gb_ref.at[u - DOWN], 32, thirds),
            (u == LAST, wd_ref.at[u - DOWN], gb_ref.at[u - DOWN], 32, whole),
        )

    def pair_copies(u):
        e = u - FRONT
        rows = rows_of(me, 0, 4, 128)
        out = []
        for src, cols, numbers in ((wg_ref, left, (0, 1, 2)), (wu_ref, right, (5, 6, 9))):
            for number, device in zip(numbers, (nbr_x, nbr_y, nbr_p)):
                out.append(copy(u, number, src.at[e, :, my_half], ga_ref.at[u, rows, cols], device))
        return out

    def own_copies(u, src, dst, quarter, share):
        first, count = share[:2]
        part = src.at[pl.ds(pl.multiple_of(first * quarter, quarter), count * quarter)]
        to = dst.at[rows_of(me, first, count, quarter)]
        return (copy(u, 0, part, to, nbr_x), copy(u, 1, part, to, nbr_y),
                copy(u, 2, src, dst.at[rows_of(me, 0, 4, quarter)], nbr_p))

    def send_own(u):
        for cond, src, dst, quarter, share in src_views(u):
            @pl.when(cond)
            def _():
                for c in own_copies(u, src, dst, quarter, share):
                    c.start()

        @pl.when(is_pair(u))
        def _():
            for c in pair_copies(u):
                c.start()

    def same(u, k, view, rows, device):
        return copy(u, k, view.at[rows], view.at[rows], device)

    def fwd_b(u, view, quarter, share):
        give, count = share[2], share[4]
        return (same(u, 3, view, rows_of(y_id, d_first, 1, quarter), nbr_x),
                same(u, 4, view, rows_of(x_id, d_first + 1, 1, quarter), nbr_y),
                same(u, 5, view, rows_of(x_id, give, count, quarter), nbr_z),
                same(u, 6, view, rows_of(y_id, give, count, quarter), nbr_z))

    def fwd_c(u, view, quarter):
        return (same(u, 9, view, rows_of(d_id, d_first, 2, quarter), nbr_z),)

    def fwd_d(u, view, quarter):
        return (same(u, 7, view, rows_of(x_id, 0, 4, quarter), nbr_p),
                same(u, 8, view, rows_of(y_id, 0, 4, quarter), nbr_p),
                same(u, 10, view, rows_of(d_id, 0, 4, quarter), nbr_p))

    def flat_fwd_b(u, view, quarter):
        return (same(u, 3, view, rows_of(y_id, 0, 2, quarter), nbr_x), same(u, 4, view, rows_of(x_id, 2, 2, quarter), nbr_y),
                same(u, 7, view, rows_of(x_id, 0, 4, quarter), nbr_p), same(u, 8, view, rows_of(y_id, 0, 4, quarter), nbr_p))

    def flat_fwd_c(u, view, quarter):
        return (same(u, 10, view, rows_of(d_id, 0, 4, quarter), nbr_p),)

    def got(u, k, view, rows):
        same(u, k, view, rows, nbr_p).wait_recv()

    def got_half(u, k, rows, cols):
        view = ga_ref.at[u, rows, cols]
        copy(u, k, view, view, nbr_p).wait_recv()

    def stage_b(u):
        for cond, view, quarter, share in views(u):
            @pl.when(cond)
            def _():
                got(u, 0, view, rows_of(x_id, share[0], share[1], quarter))
                got(u, 1, view, rows_of(y_id, share[0], share[1], quarter))
                for c in fwd_b(u, view, quarter, share):
                    c.start()

        @pl.when(is_pair(u))
        def _():
            for owner, first in ((x_id, 0), (y_id, 1)):
                got_half(u, first, rows_of(owner, 0, 4, 128), left)
                got_half(u, first + 5, rows_of(owner, 0, 4, 128), right)

        @pl.when(u == LAST)
        def _():
            got(u, 0, gb_ref.at[u - DOWN], rows_of(x_id, 0, 4, 32))
            got(u, 1, gb_ref.at[u - DOWN], rows_of(y_id, 0, 4, 32))

        for cond, view, quarter in flat_views(u):
            @pl.when(cond)
            def _():
                for c in flat_fwd_b(u, view, quarter):
                    c.start()

    def stage_c(u):
        for cond, view, quarter, share in views(u):
            @pl.when(cond)
            def _():
                got(u, 3, view, rows_of(d_id, d_first, 1, quarter))
                got(u, 4, view, rows_of(d_id, d_first + 1, 1, quarter))
                for c in fwd_c(u, view, quarter):
                    c.start()

        for cond, view, quarter in flat_views(u):
            @pl.when(cond)
            def _():
                got(u, 3, view, rows_of(d_id, 0, 2, quarter))
                got(u, 4, view, rows_of(d_id, 2, 2, quarter))
                for c in flat_fwd_c(u, view, quarter):
                    c.start()

    def stage_d(u):
        for cond, view, quarter, share in views(u):
            @pl.when(cond)
            def _():
                got(u, 5, view, rows_of(x_id, share[3], share[4], quarter))
                got(u, 6, view, rows_of(y_id, share[3], share[4], quarter))
                got(u, 9, view, rows_of(d_id, d_other, 2, quarter))
                for c in fwd_d(u, view, quarter):
                    c.start()

    px_id, py_id, pd_id = x_id + 1 - 2 * core, y_id + 1 - 2 * core, d_id + 1 - 2 * core

    def stage_e(u):
        for cond, view, quarter, share in views(u):
            @pl.when(cond)
            def _():
                got(u, 2, view, rows_of(p_id, 0, 4, quarter))
                got(u, 7, view, rows_of(px_id, 0, 4, quarter))
                got(u, 8, view, rows_of(py_id, 0, 4, quarter))
                got(u, 10, view, rows_of(pd_id, 0, 4, quarter))
                for c in fwd_b(u, view, quarter, share) + fwd_c(u, view, quarter) + fwd_d(u, view, quarter):
                    c.wait_send()
        for cond, src, dst, quarter, share in src_views(u):
            @pl.when(cond)
            def _():
                for c in own_copies(u, src, dst, quarter, share):
                    c.wait_send()

        @pl.when(is_pair(u))
        def _():
            got_half(u, 2, rows_of(p_id, 0, 4, 128), left)
            got_half(u, 9, rows_of(p_id, 0, 4, 128), right)
            for c in pair_copies(u):
                c.wait_send()

        @pl.when(u == LAST)
        def _():
            got(u, 2, gb_ref.at[u - DOWN], rows_of(p_id, 0, 4, 32))

        for cond, view, quarter in flat_views(u):
            @pl.when(cond)
            def _():
                got(u, 7, view, rows_of(px_id, 0, 4, quarter))
                got(u, 8, view, rows_of(py_id, 0, 4, quarter))
                got(u, 10, view, rows_of(pd_id, 0, 4, quarter))
                for c in flat_fwd_b(u, view, quarter) + flat_fwd_c(u, view, quarter):
                    c.wait_send()

    def load_all(copies, dst, buf, quarter):
        for i, owner in enumerate((p_id, x_id, px_id, y_id, py_id, d_id, pd_id)):
            rows = rows_of(owner, 0, 4, quarter)
            copies.append(pltpu.make_async_copy(dst.at[rows], buf.at[rows], load_sem.at[i + 2]))
        for c in copies:
            c.start()
        for c in copies:
            c.wait()

    def load(u):
        for cond, src, dst, quarter, share in src_views(u):
            buf = w_a if quarter == 128 else w_b

            @pl.when(cond)
            def _():
                load_all([pltpu.make_async_copy(src, buf.at[rows_of(me, 0, 4, quarter)], load_sem.at[0])], dst, buf, quarter)

        @pl.when(is_pair(u))
        def _():
            rows = rows_of(me, 0, 4, 128)
            load_all([pltpu.make_async_copy(wg_ref.at[u - FRONT, :, my_half], w_a.at[rows, left], load_sem.at[0]),
                      pltpu.make_async_copy(wu_ref.at[u - FRONT, :, my_half], w_a.at[rows, right], load_sem.at[1])], ga_ref.at[u], w_a, 128)

    def z_copy(src, dst, i):
        return pltpu.make_async_remote_copy(src_ref=src, dst_ref=dst, send_sem=zsend_sem.at[i], recv_sem=zrecv_sem.at[i],
                                            device_id=nbr_z, device_id_type=MESH_ID)

    route_copy = z_copy(route_ref, route_all.at[1], 0)
    rows_copy = z_copy(h_buf.at[0], h_buf.at[1], 1)
    act_copy = z_copy(u_mine.at[1], u_theirs, 2)

    send_own(jnp.int32(0))
    send_own(jnp.int32(1))
    route_copy.start()
    route_all[0] = route_ref[...]

    my_cols = pl.ds(pl.multiple_of(me * 512, 512), 512)

    def small_copies(step, cols, device):
        return [pltpu.make_async_remote_copy(src_ref=src, dst_ref=dst.at[:, cols], send_sem=ssend_sem.at[step - 1, i],
                                             recv_sem=srecv_sem.at[step - 1, i], device_id=device, device_id_type=MESH_ID)
                for i, (src, dst) in enumerate(((gains_ref, gains), (router_ref, router)))]

    for step in range(1, N_DEV):
        for c in small_copies(step, my_cols, (z, lax.rem(me + step, N_DEV))):
            c.start()
    gains[:, my_cols] = gains_ref[...]
    router[:, my_cols] = router_ref[...]
    for step in range(1, N_DEV):
        src_id = lax.rem(me + N_DEV - step, N_DEV)
        for c in small_copies(step, pl.ds(pl.multiple_of(src_id * 512, 512), 512), nbr_p):
            c.wait_recv()
    for step in range(1, N_DEV):
        for c in small_copies(step, my_cols, (z, lax.rem(me + step, N_DEV))):
            c.wait_send()
    x_load.wait()

    def gain(i):
        return gains[pl.ds(i, 1), :].astype(F32)

    def normed(values, gain_row):
        inv = lax.rsqrt(jnp.mean(values * values, axis=-1, keepdims=True) + NORM_EPS)
        return values * inv * gain_row

    CH = 16

    def norm_rows(i, _):
        rows = pl.ds(pl.multiple_of(i * CH, CH), CH)
        h_buf[0, rows, :] = normed(x_ref[rows, :].astype(F32), gain(0)).astype(BF16)
        return 0

    lax.fori_loop(0, N_ROWS // CH, norm_rows, 0)

    lane = lax.broadcasted_iota(jnp.int32, (32, 128), 1)
    pos = lax.broadcasted_iota(jnp.int32, (32, 128), 0)
    for prompt in range(N_ROWS // 32):
        key = lane - 32 * (prompt % 4)
        mask[pl.ds(32 * prompt, 32), :] = jnp.where((key >= 0) & (key <= pos) & (key < lens_ref[prompt]), 1.0, 0.0)

    def rope_rows(i, _):
        rows = pl.ds(pl.multiple_of(i * 64, 64), 64)
        cos_t, sin_t = cos_ref[...], sin_ref[...]
        for hd in range(COLS // HEAD_DIM):
            cols = pl.ds(hd * HEAD_DIM, HEAD_DIM)
            val = res[1, rows, cols].astype(BF16).astype(F32)
            q_buf[rows, cols] = (val * cos_t + pltpu.roll(val, HEAD_DIM // 2, 1) * sin_t).astype(BF16)
        return 0

    def attend(j):
        def head(hd, _):
            cols = pl.ds(pl.multiple_of(hd * HEAD_DIM, HEAD_DIM), HEAD_DIM)
            kv = pl.ds(pl.multiple_of(2 * HEAD_DIM * j + lax.div(hd, 4) * HEAD_DIM, HEAD_DIM), HEAD_DIM)
            out_cols = pl.ds(pl.multiple_of(COLS * j + hd * HEAD_DIM, HEAD_DIM), HEAD_DIM)
            for g in range(N_ROWS // 128):
                rows = pl.ds(g * 128, 128)
                s = lax.dot_general(q_buf[rows, cols], k_ref[rows, kv], (((1,), (1,)), ((), ())), preferred_element_type=F32) * ATTN_SCALE
                s = SOFT_CAP * jnp.tanh(s / SOFT_CAP)
                s = jnp.where(mask[rows, :] > 0.5, s, -1e30)
                p = jnp.exp(s - jnp.max(s, axis=-1, keepdims=True))
                p = (p / jnp.sum(p, axis=-1, keepdims=True)).astype(BF16)
                o_buf[rows, out_cols] = jnp.dot(p, v_ref[rows, kv], preferred_element_type=F32).astype(BF16)
            return 0

        lax.fori_loop(0, COLS // HEAD_DIM, head, 0)

    def mid_rows(i, _):
        rows = pl.ds(pl.multiple_of(i * CH, CH), CH)
        mid = (x_ref[rows, :].astype(F32) + normed(acc[rows, :], gain(1))).astype(BF16)
        o_buf[rows, :] = mid
        h_buf[0, rows, :] = normed(mid.astype(F32), gain(2)).astype(BF16)
        acc[rows, :] = jnp.zeros((CH, D_MODEL), F32)
        return 0

    def route():
        logits = lax.dot_general(h_buf[0], router[...], (((1,), (1,)), ((), ())), preferred_element_type=F32)
        lane = lax.broadcasted_iota(jnp.int32, logits.shape, 1)
        pr = jnp.exp(logits - jnp.max(logits, axis=-1, keepdims=True))
        pr = pr / jnp.sum(pr, axis=-1, keepdims=True)
        lane_f = lane.astype(F32)
        pick = (route_ref[:, 0:1] == lane_f) | (route_ref[:, 1:2] == lane_f)
        comb[...] = jnp.where(pick, pr, 0.0)

    def final_rows(i, _):
        rows = pl.ds(pl.multiple_of(i * CH, CH), CH)
        y_ref[rows, :] = (o_buf[rows, :].astype(F32) + normed(acc[rows, :], gain(3))).astype(BF16)
        return 0

    TILE = 256

    def tile_of(n):
        return pl.ds(pl.multiple_of(n * TILE, TILE), TILE)

    AROWS = 64

    def compute(u, side):
        @pl.when(u < FRONT)
        def _():
            def matmul(lhs):
                def tile(n, _):
                    res[1, :, tile_of(n)] = jnp.dot(lhs[...], w_a[:, tile_of(n)], preferred_element_type=F32)
                    return 0
                lax.fori_loop(0, COLS // TILE, tile, 0)

            @pl.when(u >= 6)
            def _():
                matmul(o_buf)
                acc[:, pl.ds(pl.multiple_of((u - 6) * COLS, COLS), COLS)] = res[1]

            @pl.when(u < 6)
            def _():
                matmul(h_buf.at[0])

            @pl.when((u < 6) & (u != 1))
            def _():
                lax.fori_loop(0, N_ROWS // 64, rope_rows, 0)

            @pl.when(u == 0)
            def _():
                k_ref[...] = q_buf[...]

            @pl.when(u == 1)
            def _():
                v_ref[...] = res[1].astype(BF16)

            @pl.when((u >= 2) & (u < 6))
            def _():
                attend(u - 2)

            @pl.when(u == FRONT - 1)
            def _():
                lax.fori_loop(0, N_ROWS // CH, mid_rows, 0)
                route()
                rows_copy.start()

        @pl.when(is_pair(u))
        def _():
            e_f = (u - FRONT).astype(F32)

            def tile(n, _):
                res[1, :, tile_of(n)] = jnp.dot(h_buf[side], w_a[:, tile_of(n)], preferred_element_type=F32)
                return 0
            lax.fori_loop(0, COLS // TILE, tile, 0)

            def act(n, _):
                rows = pl.ds(pl.multiple_of(n * AROWS, AROWS), AROWS)
                val = (jax.nn.gelu(res[1, rows, left]) * res[1, rows, right]).astype(BF16)
                for choice in range(2):
                    take = jnp.broadcast_to(route_all[side, rows, choice:choice + 1] == e_f, (AROWS, HALF))
                    old = u_mine[side, choice, rows, :]
                    u_mine[side, choice, rows, :] = jnp.where(take, val.astype(F32), old.astype(F32)).astype(BF16)
                return 0
            lax.fori_loop(0, N_ROWS // AROWS, act, 0)

        @pl.when(u >= DOWN)
        def _():
            e = u - DOWN
            e_f = e.astype(F32)

            other_half = pl.ds(pl.multiple_of(HALF * (1 - z), HALF), HALF)

            def spread(n, _):
                rows = pl.ds(pl.multiple_of(n * AROWS, AROWS), AROWS)
                first = jnp.broadcast_to(route_ref[rows, 0:1] == e_f, (AROWS, HALF))
                second = jnp.broadcast_to(route_ref[rows, 1:2] == e_f, (AROWS, HALF))
                for cols, picked in ((my_half, u_mine.at[0]), (other_half, u_theirs)):
                    val = jnp.where(first, picked[0, rows, :].astype(F32), jnp.where(second, picked[1, rows, :].astype(F32), 0.0))
                    u_buf[rows, cols] = val.astype(BF16)
                return 0

            lax.fori_loop(0, N_ROWS // AROWS, spread, 0)
            lane = lax.broadcasted_iota(jnp.int32, comb.shape, 1)
            weight = jnp.sum(jnp.where(lane == e, comb[...], 0.0), axis=-1, keepdims=True)

            def tile(n, _):
                out = jnp.dot(u_buf[...], w_b[:, tile_of(n)], preferred_element_type=F32)
                acc[:, tile_of(n)] += weight * out
                return 0

            lax.fori_loop(0, D_MODEL // TILE, tile, 0)

    def step(s, _):
        arrives = (s < LAST) | (s == LAST + 1)

        @pl.when(arrives)
        def _():
            stage_b(unit_at(s))

        @pl.when((s + LOOK < LAST) | (s == LAST - 1))
        def _():
            send_own(unit_at(s + LOOK))

        def work(t, _):
            u = t - steps_of(t, ((0, 0), (EARLY, 5), (THEIRS, 8)))
            side = steps_of(t, ((0, 0), (EARLY, 1), (THEIRS, 0)))

            @pl.when((t < EARLY) | ((t >= EARLY + 5) & (t < THEIRS)) | (t >= LATE))
            def _():
                stage_e(u)

            @pl.when(t == EARLY)
            def _():
                route_copy.wait_recv()
                rows_copy.wait_recv()

            load(u)

            @pl.when(t == THEIRS)
            def _():
                act_copy.start()

            @pl.when(t == LATE)
            def _():
                act_copy.wait_recv()

            compute(u, side)
            return 0

        lax.fori_loop(tasks_done(s - 1), tasks_done(s), work, 0)

        @pl.when(arrives)
        def _():
            stage_c(unit_at(s))

        def finish(place, _):
            stage_d(unit_at(place))
            return 0

        lax.fori_loop(stage_d_done(s - 1), stage_d_done(s), finish, 0)
        return 0

    lax.fori_loop(0, UNITS + LAG, step, 0)
    for c in (route_copy, rows_copy, act_copy):
        c.wait_send()
    lax.fori_loop(0, N_ROWS // CH, final_rows, 0)


def solution(mesh):
    row_spec = P(('dp', 'wg'))
    dim0_spec = P('wg', None)
    dim1_spec = P(None, 'wg', None)

    def device_fn(hidden, seq_lens, route_idx, g_attn_in, w_query, w_key, w_value, w_attn_out, g_attn_out, g_moe_in, w_router, w_gate, w_up, w_down, g_moe_out):
        n_prompts, seq_len, d_model = hidden.shape
        gains = jnp.concatenate([g_attn_in, g_attn_out, g_moe_in, g_moe_out]).reshape(4, g_attn_in.shape[0])
        rows = hidden.reshape(n_prompts * seq_len, d_model)
        cos_t, sin_t = rope_tables(seq_len, 64)
        route = jnp.pad(route_idx.astype(F32), ((0, 0), (0, 128 - route_idx.shape[1])))
        vmem = pl.BlockSpec(memory_space=pltpu.VMEM)
        hbm = pl.BlockSpec(memory_space=pl.ANY)
        y_out, k_out, v_out, _, _ = pl.pallas_call(
            layer_kernel,
            out_shape=(
                jax.ShapeDtypeStruct((N_ROWS, D_MODEL), BF16),
                jax.ShapeDtypeStruct((N_ROWS, COLS), BF16),
                jax.ShapeDtypeStruct((N_ROWS, COLS), BF16),
                jax.ShapeDtypeStruct((DOWN, D_MODEL, COLS), BF16),
                jax.ShapeDtypeStruct((N_EXP, COLS, D_MODEL), BF16),
            ),
            in_specs=[hbm] + [vmem] * 5 + [pl.BlockSpec(memory_space=pltpu.SMEM)] + [hbm] * 7,
            out_specs=(vmem, vmem, vmem, hbm, hbm),
            scratch_shapes=[
                pltpu.VMEM((2, N_ROWS, D_MODEL), BF16),
                pltpu.VMEM((N_ROWS, D_MODEL), BF16),
                pltpu.VMEM((N_ROWS, D_MODEL), F32),
                pltpu.VMEM((D_MODEL, COLS), BF16),
                pltpu.VMEM((COLS, D_MODEL), BF16),
                pltpu.VMEM((2, N_ROWS, COLS), F32),
                pltpu.VMEM((N_ROWS, COLS), BF16),
                pltpu.VMEM((N_ROWS, COLS), BF16),
                pltpu.VMEM((2, 2, N_ROWS, HALF), BF16),
                pltpu.VMEM((2, N_ROWS, HALF), BF16),
                pltpu.VMEM((N_ROWS, D_MODEL), BF16),
                pltpu.VMEM((4, D_MODEL), BF16),
                pltpu.VMEM((N_EXP, D_MODEL), BF16),
                pltpu.VMEM((N_ROWS, N_EXP), F32),
                pltpu.VMEM((N_ROWS, 128), F32),
                pltpu.VMEM((2, N_ROWS, 128), F32),
                pltpu.SemaphoreType.DMA((SLOTS, COPIES)),
                pltpu.SemaphoreType.DMA((SLOTS, COPIES)),
                pltpu.SemaphoreType.DMA((N_DEV + 1,)),
                pltpu.SemaphoreType.DMA((N_DEV - 1, 2)),
                pltpu.SemaphoreType.DMA((N_DEV - 1, 2)),
                pltpu.SemaphoreType.DMA((3,)),
                pltpu.SemaphoreType.DMA((3,)),
            ],
            compiler_params=pltpu.CompilerParams(collective_id=0, has_side_effects=True, vmem_limit_bytes=62 * 1024 * 1024),
        )(rows, gains, w_router.T, jnp.asarray(cos_t), jnp.asarray(sin_t), route, seq_lens, w_query, w_key, w_value, w_attn_out, w_gate, w_up, w_down)
        cache_shape = (n_prompts, seq_len, COLS // HEAD_DIM, HEAD_DIM)
        return y_out.reshape(hidden.shape), k_out.reshape(cache_shape), v_out.reshape(cache_shape)

    return jax.shard_map(
        device_fn,
        mesh=mesh,
        in_specs=(row_spec, row_spec, row_spec, P('wg'), dim0_spec, dim0_spec, dim0_spec, dim0_spec, P('wg'), P('wg'), dim0_spec, dim1_spec, dim1_spec, dim1_spec, P('wg')),
        out_specs=(row_spec, row_spec, row_spec),
        check_vma=False,
    )
```

time: 1390 us -> 765 us (0.55)
  waiting for transfers between devices: 930 us -> 0 us
  Pallas kernels: 0 us -> 752 us
  matrix products: 321 us -> 0 us
  local copies, waits for them, and re-layouts: 77.1 us -> 11.1 us
  other arithmetic: 30.3 us -> 1.43 us
  between operations: 14.7 us -> 0.65 us
    all_gather x16 -> x0, waiting for transfers between devices: 929 us -> none  [half_gather(): return lax.all_gather(part, ('wg', 'dp'), axis=axis, tiled=True)]
    pallas_call x0 -> x1, Pallas kernels: none -> 752 us  [device_fn(): pl.pallas_call(layer_kernel, out_shape=(jax.ShapeDtypeStruct((N_ROWS, D_M...]
    dot_general x24 -> x0, matrix products: 321 us -> none  [the longest x21 311 us: dot_f32(): return jnp.dot(left_op, right_op, preferred_element_type=jnp.float32)]
    dynamic_slice x16 -> x0, local copies, waits for them, and re-layouts: 30.5 us -> none  [half_gather(): lax.dynamic_slice_in_dim(shard, lax.axis_index('dp') * n, n, axis=axis)]
    slice x6 -> x0, local copies, waits for them, and re-layouts: 19 us -> none  [the longest x1 5.69 us: device_fn(): wd_ = half_gather(w_down[e0:e0 + step], 1)]
    convert_element_type x3 -> x1, other arithmetic: 15.1 us -> 0.69 us  [device_fn(): route_idx.astype(F32)]
  transfers between devices with their start and end apart: 16 -> 0, of which waited for: 15 -> 0; matrix products, arithmetic and copies ran while one was open for 26% -> 0% of each run, Pallas kernels for 0% -> 0%
where the time goes in v2:
time: 765 us
  Pallas kernels  752 us (98%)
  local copies, waits for them, and re-layouts  11.1 us (1%)
    pallas_call x1, Pallas kernels, device_fn(): pl.pallas_call(layer_kernel, out_shape=(jax.ShapeDtypeStruct((N_ROWS, D_M...  752 us

profile of v2, /device:TPU:0, one launch (start us, length us, event | category | flops | bytes accessed | tf_op | source)
XLA Modules:
  0.0 764.8 jit_solution(1139326027462471153)
XLA Ops:
  0.6 0.7 convert_element_type.5
  1.3 0.7 pad_maximum_fusion
  2.1 0.6 reshape.22.gains_ref
  2.7 0.1 copy.21
  2.8 0.7 pad.4.route_ref
  3.5 751.6 %shard_map.184 = (bf16[512,4096]{1,0:T(8,128)(2,1)}, bf16[512,1024]{1,0:T(8,128)(2,1)}, bf16[512,1024]{1,0:T(8,128)(2,1)}, bf16[18,4096,1024]{2,1,0:T(8,128)(2,1)}, bf16[8,1024,4096]{2,1,0:T(8,128)(2,1)}) custom-call(bf16[512,4096]{1,0:T(8,128)(2,1)} %bitcast.9, bf16[4,512]{1,0:T(4,128)(2,1)} %reshape.22.gains_ref, bf16[8,512]{1,0:T(8,128)(2,1)} %bitcast.15, ...), custom_call_target="tpu_custom_call" | custom-call | tf_op jit(solution)/shard_map/pallas_call | solution.py:574
  755.2 2.5 copy.22
  757.7 2.5 copy.23
  760.1 4.7 copy.25

commit v3 on v2

--- a/solution.py
+++ b/solution.py
@@ -27,7 +27,7 @@
 UNITS = DOWN + N_EXP
 COPIES = 11
 SLOTS = 18
-HALVES = 8
+HALVES = 6
 LAST = UNITS - 1
 SOON = 10
 LOOK = 2

time: 765 us -> 767 us (level)
  no operation moved by 1% of the time
where the time goes in v3:
time: 767 us
  Pallas kernels  754 us (98%)
  local copies, waits for them, and re-layouts  11.1 us (1%)
    pallas_call x1, Pallas kernels, device_fn(): pl.pallas_call(layer_kernel, out_shape=(jax.ShapeDtypeStruct((N_ROWS, D_M...  754 us

profile of v3, /device:TPU:0, one launch (start us, length us, event | category | flops | bytes accessed | tf_op | source)
XLA Modules:
  0.0 766.7 jit_solution(14211869998045576048)
XLA Ops:
  0.6 0.7 convert_element_type.5
  1.3 0.7 pad_maximum_fusion
  2.1 0.6 reshape.22.gains_ref
  2.7 0.1 copy.21
  2.8 0.7 pad.4.route_ref
  3.5 753.5 %shard_map.184 = (bf16[512,4096]{1,0:T(8,128)(2,1)}, bf16[512,1024]{1,0:T(8,128)(2,1)}, bf16[512,1024]{1,0:T(8,128)(2,1)}, bf16[18,4096,1024]{2,1,0:T(8,128)(2,1)}, bf16[8,1024,4096]{2,1,0:T(8,128)(2,1)}) custom-call(bf16[512,4096]{1,0:T(8,128)(2,1)} %bitcast.9, bf16[4,512]{1,0:T(4,128)(2,1)} %reshape.22.gains_ref, bf16[8,512]{1,0:T(8,128)(2,1)} %bitcast.15, ...), custom_call_target="tpu_custom_call" | custom-call | tf_op jit(solution)/shard_map/pallas_call | solution.py:574
  757.1 2.5 copy.22
  759.5 2.5 copy.23
  762.0 4.7 copy.25
